TPU v7x, 32 devices: a whole 2x2x4 slice. The times are simulated.
32 devices in a mesh: dp: 4 (over z), expert: 8 (over y, x, core).
Axes of the slice: x: 2, y: 2, z: 4, core: 2. Of those that a mesh axis runs over, the one named last changes fastest.
Arguments:
- tokens: bfloat16 [2, 12288, 768], P(None, ('dp', 'expert')), may hold values from -6 to 6
- cotangent: bfloat16 [2, 12288, 768], P(None, ('dp', 'expert')), may hold values from -6 to 6
- token_ids: int32 [2, 12288], P(None, ('dp', 'expert')), may hold values from 0 to 8007, as said below
- hash_table: int32 [8008], replicated, may hold values from 0 to 7, as said below
- segment_ids: int32 [2, 12288], P(None, ('dp', 'expert')), may hold values from 0 to 1, as said below
- query_weight: bfloat16 [768, 768], replicated, may hold values from -0.21875 to 0.21875
- key_weight: bfloat16 [768, 768], replicated, may hold values from -0.21875 to 0.21875
- value_weight: bfloat16 [768, 768], replicated, may hold values from -0.21875 to 0.21875
- output_weight: bfloat16 [768, 768], replicated, may hold values from -2.5 to 2.5
- gain_attn: float32 [768], replicated, may hold values from 0.5 to 1.5
- gain_ffn: float32 [768], replicated, may hold values from 0.5 to 1.5
- expert_in: bfloat16 [8, 768, 3072], P('expert'), may hold values from -0.21875 to 0.21875
- expert_out: bfloat16 [8, 3072, 768], P('expert'), may hold values from -0.109375 to 0.109375
Outputs:
- block_out: bfloat16 [2, 12288, 768], P(None, ('dp', 'expert'))
- grad_tokens: bfloat16 [2, 12288, 768], P(None, ('dp', 'expert'))
- grad_query: float32 [768, 768], replicated
- grad_key: float32 [768, 768], replicated
- grad_value: float32 [768, 768], replicated
- grad_output: float32 [768, 768], replicated
- grad_gain_attn: float32 [768], replicated
- grad_gain_ffn: float32 [768], replicated
- grad_expert_in: float32 [8, 768, 3072], P('expert')
- grad_expert_out: float32 [8, 3072, 768], P('expert')
Inputs may be any that keep to these rules, and one draw needn't show every extreme that they name: hash_table sends 8008 // 8 or more ids to every expert. `token_ids`: in every micro-batch the 384 tokens of one device name any expert, through hash_table, at most 96 times; in every micro-batch one expert is named exactly 96 times by the tokens of every device. `segment_ids`: in each micro-batch a device's block holds either one sequence (all 0) or a sequence of 256 tokens (0) followed by one of the rest (1).
All inputs are finite; a program needn't handle non-finite values.
Results may differ from a plain program's by a relative error of at most 0.012.
Values may be sent and summed in bfloat16 or wider, within the bound.
No kernel may reach another device: no remote copies, remote signals or barrier semaphores. Data moves between devices by JAX's collectives and lax.ppermute only.
A program may use at most 192 MiB of HBM per device.

v0:
```python
import jax
import jax.numpy as jnp
from jax import lax
from jax.sharding import PartitionSpec as P

HEADS = 12
HEAD_DIM = 64
epsilon = 1e-05


def normalize(values, gain):
    return values * lax.rsqrt(jnp.mean(values * values, axis=-1, keepdims=True) + epsilon) * gain


def smooth_slope(values):
    sigmoid_part = jax.nn.sigmoid(values)
    return sigmoid_part * (1.0 + values * (1.0 - sigmoid_part))


def split_heads(matrix, head_count):
    return matrix.reshape(matrix.shape[0], head_count, -1).transpose(1, 0, 2)


def merge_heads(tensor):
    return tensor.transpose(1, 0, 2).reshape(tensor.shape[1], -1)


def masked_scores(query_heads, key_heads, allowed, score_scale):
    scores = (
        jnp.einsum("hqd,hkd->hqk", query_heads, key_heads, preferred_element_type=jnp.float32)
        * score_scale
    )
    return jnp.where(allowed[None], scores, -1e30)


def per_device(
    tokens,
    cotangent,
    token_ids,
    hash_table,
    segment_ids,
    query_weight,
    key_weight,
    value_weight,
    output_weight,
    gain_attn,
    gain_ffn,
    expert_in,
    expert_out,
):
    batches = tokens.shape[0]
    length = tokens.shape[1]
    model_width = tokens.shape[2]
    owners = lax.axis_size("expert")
    capacity = 2 * length // owners
    head_count = HEADS
    score_scale = HEAD_DIM ** (-0.5)
    weight_in = expert_in[0]
    weight_out = expert_out[0]
    position = jnp.arange(length, dtype=jnp.int32)
    float_type = jnp.float32
    half_type = jnp.bfloat16
    dense_total = (
        jnp.zeros(query_weight.shape, float_type),
        jnp.zeros(key_weight.shape, float_type),
        jnp.zeros(value_weight.shape, float_type),
        jnp.zeros(output_weight.shape, float_type),
        jnp.zeros(gain_attn.shape, float_type),
        jnp.zeros(gain_ffn.shape, float_type),
    )
    grad_in_sum = jnp.zeros(weight_in.shape, float_type)
    grad_out_sum = jnp.zeros(weight_out.shape, float_type)
    outputs = []
    grads_in = []
    for batch in range(batches):
        inputs_f = tokens[batch].astype(float_type)
        segments = segment_ids[batch]
        allowed = (position[:, None] >= position[None, :]) & (
            segments[:, None] == segments[None, :]
        )
        normed_attn = normalize(inputs_f, gain_attn).astype(half_type)
        query_heads = split_heads(
            jnp.dot(normed_attn, query_weight, preferred_element_type=float_type).astype(half_type),
            head_count,
        )
        key_heads = split_heads(
            jnp.dot(normed_attn, key_weight, preferred_element_type=float_type).astype(half_type),
            head_count,
        )
        value_heads = split_heads(
            jnp.dot(normed_attn, value_weight, preferred_element_type=float_type).astype(half_type),
            head_count,
        )
        scores = masked_scores(query_heads, key_heads, allowed, score_scale)
        row_peak = jnp.max(scores, axis=-1, keepdims=True)
        log_total = row_peak + jnp.log(jnp.sum(jnp.exp(scores - row_peak), axis=-1, keepdims=True))
        probs_low = jnp.exp(scores - log_total).astype(half_type)
        attended = merge_heads(
            jnp.einsum("hqk,hkd->hqd", probs_low, value_heads, preferred_element_type=float_type)
        ).astype(half_type)
        hidden = inputs_f + jnp.dot(attended, output_weight, preferred_element_type=float_type)
        routed = normalize(hidden, gain_ffn).astype(half_type)
        experts = jnp.take(hash_table, token_ids[batch])
        onehot = (experts[:, None] == jnp.arange(owners, dtype=jnp.int32)[None, :]).astype(
            jnp.int32
        )
        rank = jnp.sum((jnp.cumsum(onehot, axis=0, dtype=jnp.int32) - onehot) * onehot, axis=1)
        slot_index = experts * capacity + rank
        packed = jnp.zeros((owners * capacity, model_width), half_type).at[slot_index].set(routed)
        packed = packed.reshape(owners, capacity, model_width)
        received = lax.all_to_all(
            packed, "expert", split_axis=0, concat_axis=0, tiled=True
        ).reshape(owners * capacity, model_width)
        pre_active = jnp.dot(received, weight_in, preferred_element_type=float_type)
        active = jax.nn.silu(pre_active).astype(half_type)
        produced = jnp.dot(active, weight_out, preferred_element_type=float_type).astype(half_type)
        returned = lax.all_to_all(
            produced.reshape(owners, capacity, model_width),
            "expert",
            split_axis=0,
            concat_axis=0,
            tiled=True,
        )
        returned = returned.reshape(owners * capacity, model_width)
        block_out = hidden + jnp.take(returned, slot_index, axis=0).astype(float_type)
        outputs.append(block_out.astype(half_type))
        grad_block = cotangent[batch].astype(float_type)
        grad_result = grad_block.astype(half_type)
        grad_packed = (
            jnp.zeros((owners * capacity, model_width), half_type).at[slot_index].set(grad_result)
        )
        grad_packed = grad_packed.reshape(owners, capacity, model_width)
        grad_recv = lax.all_to_all(grad_packed, "expert", split_axis=0, concat_axis=0, tiled=True)
        grad_recv = grad_recv.reshape(owners * capacity, model_width)
        slope = smooth_slope(pre_active)
        grad_out_sum = grad_out_sum + jnp.dot(
            active.T, grad_recv, preferred_element_type=float_type
        )
        grad_active = jnp.dot(grad_recv, weight_out.T, preferred_element_type=float_type)
        grad_pre = (grad_active * slope).astype(half_type)
        grad_in_sum = grad_in_sum + jnp.dot(received.T, grad_pre, preferred_element_type=float_type)
        grad_rows = jnp.dot(grad_pre, weight_in.T, preferred_element_type=float_type).astype(
            half_type
        )
        grad_back = lax.all_to_all(
            grad_rows.reshape(owners, capacity, model_width),
            "expert",
            split_axis=0,
            concat_axis=0,
            tiled=True,
        )
        grad_routed = jnp.take(
            grad_back.reshape(owners * capacity, model_width), slot_index, axis=0
        ).astype(float_type)
        ignored_ffn, pull_ffn = jax.vjp(normalize, hidden, gain_ffn)
        grad_from_ffn, grad_gain_two = pull_ffn(grad_routed)
        grad_hidden = grad_block + grad_from_ffn
        grad_attn = grad_hidden.astype(half_type)
        grad_output_term = jnp.dot(attended.T, grad_attn, preferred_element_type=float_type)
        grad_mixed = split_heads(
            jnp.dot(grad_attn, output_weight.T, preferred_element_type=float_type).astype(
                half_type
            ),
            head_count,
        )
        scores_again = masked_scores(query_heads, key_heads, allowed, score_scale)
        probs = jnp.exp(scores_again - log_total)
        probs_again = probs.astype(half_type)
        grad_values = jnp.einsum(
            "hqk,hqd->hkd", probs_again, grad_mixed, preferred_element_type=float_type
        ).astype(half_type)
        grad_probs = jnp.einsum(
            "hqd,hkd->hqk", grad_mixed, value_heads, preferred_element_type=float_type
        )
        shared = jnp.sum(probs * grad_probs, axis=-1, keepdims=True)
        grad_scores = (probs * (grad_probs - shared)).astype(half_type)
        grad_queries = (
            jnp.einsum("hqk,hkd->hqd", grad_scores, key_heads, preferred_element_type=float_type)
            * score_scale
        ).astype(half_type)
        grad_keys = (
            jnp.einsum("hqk,hqd->hkd", grad_scores, query_heads, preferred_element_type=float_type)
            * score_scale
        ).astype(half_type)
        grad_queries = merge_heads(grad_queries)
        grad_keys = merge_heads(grad_keys)
        grad_values = merge_heads(grad_values)
        grad_query_term = jnp.dot(normed_attn.T, grad_queries, preferred_element_type=float_type)
        grad_key_term = jnp.dot(normed_attn.T, grad_keys, preferred_element_type=float_type)
        grad_value_term = jnp.dot(normed_attn.T, grad_values, preferred_element_type=float_type)
        grad_normed = (
            jnp.dot(grad_queries, query_weight.T, preferred_element_type=float_type)
            + jnp.dot(grad_keys, key_weight.T, preferred_element_type=float_type)
            + jnp.dot(grad_values, value_weight.T, preferred_element_type=float_type)
        )
        ignored_attn, pull_attn = jax.vjp(normalize, inputs_f, gain_attn)
        grad_from_attn, grad_gain_one = pull_attn(grad_normed)
        grads_in.append((grad_hidden + grad_from_attn).astype(half_type))
        terms = (
            grad_query_term,
            grad_key_term,
            grad_value_term,
            grad_output_term,
            grad_gain_one,
            grad_gain_two,
        )
        dense_total = tuple((total + term for total, term in zip(dense_total, terms)))
    dense_total = lax.psum(
        (
            dense_total[0],
            dense_total[1],
            dense_total[2],
            dense_total[3],
            dense_total[4],
            dense_total[5],
        ),
        ("dp", "expert"),
    )
    expert_in_sum, expert_out_sum = (
        lax.psum(grad_in_sum.astype(jnp.bfloat16), "dp").astype(jnp.float32),
        lax.psum(grad_out_sum.astype(jnp.bfloat16), "dp").astype(jnp.float32),
    )
    return (
        jnp.stack(outputs),
        jnp.stack(grads_in),
        dense_total[0],
        dense_total[1],
        dense_total[2],
        dense_total[3],
        dense_total[4],
        dense_total[5],
        expert_in_sum[None],
        expert_out_sum[None],
    )


def solution(mesh):
    placed = (
        P(None, ("dp", "expert"), None),
        P(None, ("dp", "expert"), None),
        P(None, ("dp", "expert")),
        P(),
        P(None, ("dp", "expert")),
        P(),
        P(),
        P(),
        P(),
        P(),
        P(),
        P("expert", None, None),
        P("expert", None, None),
    )
    return jax.shard_map(
        per_device,
        mesh=mesh,
        in_specs=placed,
        out_specs=(
            P(None, ("dp", "expert"), None),
            P(None, ("dp", "expert"), None),
            P(),
            P(),
            P(),
            P(),
            P(),
            P(),
            P("expert", None, None),
            P("expert", None, None),
        ),
        check_vma=False,
    )
```

profile of v0, /device:TPU:0, one launch (start us, length us, event | category | flops | bytes accessed | tf_op | source)
XLA Modules:
  0.0 789.7 jit_solution(1991907835853382940)
XLA Ops:
  17.7 3.0 convolution_convert_fusion.10
  22.1 2.4 fusion
  31.8 2.5 gather_fusion
  36.2 3.9 scatter_custom_fusion
  40.1 5.7 all-to-all-start
  60.4 2.5 gather_fusion.2
  63.0 5.8 convolution_convert_fusion
  72.9 3.2 scatter_custom_fusion.1
  76.1 4.3 all-to-all-start.2
  80.5 3.3 scatter_custom_fusion.2
  83.8 3.1 scatter_custom_fusion.3
  88.1 9.2 %all-to-all-done.2 = bf16[8,96,768]{2,1,0:T(8,128)(2,1)S(1)} async-done(((bf16[8,96,768]{2,1,0:T(8,128)(2,1)}), bf16[8,96,768]{2,1,0:T(8,128)(2,1)S(1)}, u32[]{:S(2)}, u32[]{:S(2)}) %all-to-all-start.2) | async-done | bytes 1179680 | tf_op jit(solution)/shard_map/all_to_all | solution.py:111
  97.3 3.6 all-to-all-start.4
  100.9 12.6 %multiply_convert_fusion.3 = (bf16[768,3072]{1,0:T(8,128)(2,1)}, f32[768,3072]{1,0:T(8,128)}) fusion(bf16[768,768]{1,0:T(8,128)(2,1)} %bitcast.13, bf16[1,768,3072]{2,1,0:T(8,128)(2,1)} %param.28), kind=kOutput, calls=%fused_computation.16 | convolution fusion | flops 3635675136 | bytes 20054016 | tf_op jit(solution)/shard_map/dot_general | solution.py:114
  113.5 8.5 %fusion.12 = f32[768,3072]{1,0:T(8,128)} fusion(bf16[768,768]{1,0:T(8,128)(2,1)S(1)} %bitcast.311, bf16[1,768,3072]{2,1,0:T(8,128)(2,1)} %param.28), kind=kOutput, calls=%fused_computation.40 | convolution fusion | flops 3623878656 | bytes 15335424 | tf_op jit(solution)/shard_map/dot_general | solution.py:114
  122.0 4.1 all-to-all-start.6
  126.1 8.8 %multiply_convert_fusion.1 = bf16[768,3072]{1,0:T(8,128)(2,1)S(1)} fusion(f32[768,3072]{1,0:T(8,128)} %get-tuple-element.57, bf16[768,768]{1,0:T(8,128)(2,1)S(1)} %bitcast.314, bf16[1,3072,768]{2,1,0:T(8,128)(2,1)} %param.29), kind=kOutput, calls=%fused_computation.13 | convolution fusion | flops 3645112320 | bytes 20054016 | tf_op jit(solution)/shard_map/dot_general | solution.py:139
  135.0 10.2 %fusion.145 = f32[3072,768]{1,0:T(8,128)} fusion(bf16[768,3072]{1,0:T(8,128)(2,1)} %get-tuple-element.56, bf16[768,768]{1,0:T(8,128)(2,1)S(1)} %bitcast.315), kind=kOutput, calls=%fused_computation.230 | convolution fusion | flops 3623878656 | bytes 15335424 | tf_op jit(solution)/shard_map/dot_general | solution.py:136
  145.2 7.2 fusion.20
  152.4 4.4 all-to-all-start.5
  156.9 8.9 %multiply_convert_fusion = bf16[768,3072]{1,0:T(8,128)(2,1)S(1)} fusion(f32[768,3072]{1,0:T(8,128)} %fusion.12, bf16[768,768]{1,0:T(8,128)(2,1)S(1)} %bitcast.316, bf16[1,3072,768]{2,1,0:T(8,128)(2,1)} %param.29), kind=kOutput, calls=%fused_computation.12 | convolution fusion | flops 3645112320 | bytes 20054016 | tf_op jit(solution)/shard_map/dot_general | solution.py:139
  165.8 15.0 %fusion.17 = bf16[1,3072,768]{2,1,0:T(8,128)(2,1)} fusion(f32[3072,768]{1,0:T(8,128)} %fusion.145, bf16[768,768]{1,0:T(8,128)(2,1)S(1)} %bitcast.317, f32[768,3072]{1,0:T(8,128)} %fusion.12), kind=kOutput, calls=%fused_computation.45 | convolution fusion | flops 3640393728 | bytes 24772608 | tf_op jit(solution)/shard_map/dot_general | solution.py:136
  180.9 4.9 fusion.23
  185.7 4.6 all-to-all-start.7
  190.4 11.1 %fusion.29 = bf16[768,768]{1,0:T(8,128)(2,1)} fusion(bf16[1,3072,768]{2,1,0:T(8,128)(2,1)} %param.29, f32[768,3072]{1,0:T(8,128)} %fusion.12), kind=kOutput, calls=%fused_computation.59 | convolution fusion | flops 3636264960 | bytes 15335424 | tf_op jit(solution)/shard_map/dot_general | solution.py:116
  201.4 5.7 all-to-all-done.7
  207.2 4.3 all-to-all-start.3
  211.4 10.3 %fusion.144 = f32[768,3072]{1,0:T(8,128)} fusion(bf16[768,768]{1,0:T(8,128)(2,1)} %bitcast.13, bf16[768,3072]{1,0:T(8,128)(2,1)} %copy-done.26), kind=kOutput, calls=%fused_computation.229 | convolution fusion | flops 3623878656 | bytes 15335424 | tf_op jit(solution)/shard_map/dot_general | solution.py:141
  221.8 8.6 %fusion.26 = bf16[768,768]{1,0:T(8,128)(2,1)} fusion(bf16[768,3072]{1,0:T(8,128)(2,1)} %get-tuple-element.56, bf16[1,3072,768]{2,1,0:T(8,128)(2,1)} %param.29), kind=kOutput, calls=%fused_computation.58 | convolution fusion | flops 3624468480 | bytes 10616832 | tf_op jit(solution)/shard_map/dot_general | solution.py:116
  230.4 4.3 all-to-all-start.1
  234.9 11.5 %fusion.16 = bf16[1,768,3072]{2,1,0:T(8,128)(2,1)} fusion(f32[768,3072]{1,0:T(8,128)} %fusion.144, bf16[768,768]{1,0:T(8,128)(2,1)} %bitcast.312, bf16[768,3072]{1,0:T(8,128)(2,1)} %copy-done.92), kind=kOutput, calls=%fused_computation.44 | convolution fusion | flops 3628597248 | bytes 20054016 | tf_op jit(solution)/shard_map/dot_general | solution.py:141
  247.1 2.6 gather_fusion.5
  249.7 4.4 gather_fusion.3
  254.2 2.6 gather_fusion.4
  256.9 3.1 fusion.60
  260.6 4.4 gather_fusion.1
  265.0 4.2 fusion.70
  272.9 2.8 convolution_convert_fusion.5
  277.9 5.6 multiply_reduce_fusion.1
  298.3 2.4 multiply_convert_fusion.4
  321.8 2.6 fusion.57
  325.5 46.7 %all-reduce = (f32[768]{0:T(1024)}, f32[768]{0:T(1024)}) all-reduce(f32[768]{0:T(1024)} %add.207, f32[768]{0:T(1024)} %add.208), channel_id=1, replica_groups=mesh['dp'=4,'expert'=8] {'dp','expert'}, use_global_device_ids=true, to_apply=%region_30.33 | all-reduce | flops 1536 | bytes 12288 | tf_op jit(solution)/shard_map/psum | solution.py:208
  372.2 2.5 pad_maximum_fusion
  378.5 196.6 %all-reduce.8.cloned.1.call-done = (bf16[1,768,3072]{2,1,0:T(8,128)(2,1)}, bf16[1,3072,768]{2,1,0:T(8,128)(2,1)}) async-done(((bf16[1,768,3072]{2,1,0:T(8,128)(2,1)}, bf16[1,3072,768]{2,1,0:T(8,128)(2,1)}), (bf16[1,768,3072]{2,1,0:T(8,128)(2,1)}, bf16[1,3072,768]{2,1,0:T(8,128)(2,1)})) %all-reduce.8.cloned.1.call-update) | async-done | bytes 9437200 | tf_op jit(solution)/shard_map/psum | solution.py:220
  575.1 7.5 broadcast_in_dim.117
  582.6 4.9 broadcast_in_dim.119
  587.5 185.4 %all-reduce.6.cloned.1.call-done = (f32[768,768]{1,0:T(8,128)}, f32[768,768]{1,0:T(8,128)}, f32[768,768]{1,0:T(8,128)}, f32[768,768]{1,0:T(8,128)}) async-done(((f32[768,768]{1,0:T(8,128)}, f32[768,768]{1,0:T(8,128)}, f32[768,768]{1,0:T(8,128)}, f32[768,768]{1,0:T(8,128)}), (f32[768,768]{1,0:T(8,128)}, f32[768,768]{1,0:T(8,128)}, f32[768,768]{1,0:T(8,128)}, ...) | async-done | bytes 9437200 | tf_op jit(solution)/shard_map/psum | solution.py:208
  772.8 3.4 copy.69
  (293 shorter events, 94.8 us)
Async XLA Ops:
  8.9 36.9 %copy-start.79 = (f32[384]{0:T(512)}, f32[384]{0:T(512)S(1)}, u32[]{:S(2)}) copy-start(f32[384]{0:T(512)S(1)} %get-tuple-element.23) | copy-start | bytes 4612
  9.5 8.2 %copy-start.69 = (f32[384]{0:T(512)}, f32[384]{0:T(512)S(1)}, u32[]{:S(2)}) copy-start(f32[384]{0:T(512)S(1)} %fusion.115) | copy-start | bytes 4612
  11.0 3.8 copy-start.30
  17.7 4.4 copy-start.11
  24.5 2.9 copy-start.2
  26.0 3.4 copy-start.60
  31.1 5.1 copy-start.67
  31.7 8.4 %copy-start.73 = (f32[384]{0:T(512)}, f32[384]{0:T(512)S(1)}, u32[]{:S(2)}) copy-start(f32[384]{0:T(512)S(1)} %fusion.116) | copy-start | bytes 4612
  36.2 4.0 copy-start.89
  40.1 36.0 %all-to-all-start = ((bf16[8,96,768]{2,1,0:T(8,128)(2,1)}), bf16[8,96,768]{2,1,0:T(8,128)(2,1)}, u32[]{:S(2)}, u32[]{:S(2)}) async-start(bf16[8,96,768]{2,1,0:T(8,128)(2,1)} %bitcast.300), calls=%async_computation | async-start | bytes 2359296 | tf_op jit(solution)/shard_map/all_to_all | solution.py:111
  51.3 11.7 %copy-start.40 = (pred[384,384]{0,1:T(8,128)(4,1)}, pred[384,384]{0,1:T(8,128)(4,1)S(1)}, u32[]{:S(2)}) copy-start(pred[384,384]{0,1:T(8,128)(4,1)S(1)} %fusion.96) | copy-start | bytes 442372
  52.8 4.7 copy-start.15
  57.5 2.9 copy-start.3
  60.4 8.4 %copy-start.63 = (f32[12,384]{1,0:T(8,128)}, f32[12,384]{1,0:T(8,128)S(1)}, u32[]{:S(2)}) copy-start(f32[12,384]{1,0:T(8,128)S(1)} %log_add_fusion) | copy-start | bytes 55300
  72.2 3.9 copy-start.10
  72.2 3.9 copy-start.75
  76.1 4.4 copy-start.27
  76.1 4.4 copy-start.90
  76.1 21.2 %all-to-all-start.2 = ((bf16[8,96,768]{2,1,0:T(8,128)(2,1)}), bf16[8,96,768]{2,1,0:T(8,128)(2,1)S(1)}, u32[]{:S(2)}, u32[]{:S(2)}) async-start(bf16[8,96,768]{2,1,0:T(8,128)(2,1)} %bitcast.31), calls=%async_computation.2 | async-start | bytes 2359296 | tf_op jit(solution)/shard_map/all_to_all | solution.py:111
  97.3 16.2 %copy-start.54 = (bf16[8,96,768]{2,1,0:T(8,128)(2,1)}, bf16[8,96,768]{2,1,0:T(8,128)(2,1)S(1)}, u32[]{:S(2)}) copy-start(bf16[8,96,768]{2,1,0:T(8,128)(2,1)S(1)} %all-to-all-done.2) | copy-start | bytes 3538948
  97.3 24.7 %all-to-all-start.4 = ((bf16[8,96,768]{2,1,0:T(8,128)(2,1)}), bf16[8,96,768]{2,1,0:T(8,128)(2,1)S(1)}, u32[]{:S(2)}, u32[]{:S(2)}) async-start(bf16[8,96,768]{2,1,0:T(8,128)(2,1)} %bitcast.37), calls=%async_computation.4 | async-start | bytes 2359296 | tf_op jit(solution)/shard_map/all_to_all | solution.py:133
  122.0 30.4 %all-to-all-start.6 = ((bf16[8,96,768]{2,1,0:T(8,128)(2,1)}), bf16[8,96,768]{2,1,0:T(8,128)(2,1)S(1)}, u32[]{:S(2)}, u32[]{:S(2)}) async-start(bf16[8,96,768]{2,1,0:T(8,128)(2,1)} %bitcast.55), calls=%async_computation.6 | async-start | bytes 2359296 | tf_op jit(solution)/shard_map/all_to_all | solution.py:133
  134.9 10.3 %copy-start.26 = (bf16[768,3072]{1,0:T(8,128)(2,1)}, bf16[768,3072]{1,0:T(8,128)(2,1)S(1)}, u32[]{:S(2)}) copy-start(bf16[768,3072]{1,0:T(8,128)(2,1)S(1)} %multiply_convert_fusion.1) | copy-start | bytes 14155780
  152.4 33.3 %all-to-all-start.5 = ((bf16[8,96,768]{2,1,0:T(8,128)(2,1)}), bf16[8,96,768]{2,1,0:T(8,128)(2,1)S(1)}, u32[]{:S(2)}, u32[]{:S(2)}) async-start(bf16[8,96,768]{2,1,0:T(8,128)(2,1)} %bitcast.319), calls=%async_computation.5 | async-start | bytes 2359296 | tf_op jit(solution)/shard_map/all_to_all | solution.py:145
  156.8 24.0 %slice-start.4 = ((s8[4718592]{0:T(1024)(128)(4,1)}), s8[4194304]{0:T(1024)(128)(4,1)S(1)}, s32[]{:S(2)}) async-start(s8[4718592]{0:T(1024)(128)(4,1)} %bitcast.331), calls=%async_computation.14 | async-start | bytes 8388608
  165.8 15.0 %copy-start.92 = (bf16[768,3072]{1,0:T(8,128)(2,1)}, bf16[768,3072]{1,0:T(8,128)(2,1)S(1)}, u32[]{:S(2)}) copy-start(bf16[768,3072]{1,0:T(8,128)(2,1)S(1)} %multiply_convert_fusion) | copy-start | bytes 14155780
  165.8 15.0 %slice-start.5 = ((s8[4718592]{0:T(1024)(128)(4,1)}), s8[524288]{0:T(1024)(128)(4,1)S(1)}, s32[]{:S(2)}) async-start(s8[4718592]{0:T(1024)(128)(4,1)} %bitcast.331), calls=%async_computation.15 | async-start | bytes 1048576
  185.7 21.4 %all-to-all-start.7 = ((bf16[8,96,768]{2,1,0:T(8,128)(2,1)}), bf16[8,96,768]{2,1,0:T(8,128)(2,1)S(1)}, u32[]{:S(2)}, u32[]{:S(2)}) async-start(bf16[8,96,768]{2,1,0:T(8,128)(2,1)} %bitcast.320), calls=%async_computation.7 | async-start | bytes 2359296 | tf_op jit(solution)/shard_map/all_to_all | solution.py:145
  207.2 23.2 %all-to-all-start.3 = ((bf16[8,96,768]{2,1,0:T(8,128)(2,1)}), bf16[8,96,768]{2,1,0:T(8,128)(2,1)}, u32[]{:S(2)}, u32[]{:S(2)}) async-start(bf16[8,96,768]{2,1,0:T(8,128)(2,1)} %bitcast.318), calls=%async_computation.3 | async-start | bytes 2359296 | tf_op jit(solution)/shard_map/all_to_all | solution.py:117
  230.4 30.2 %all-to-all-start.1 = ((bf16[8,96,768]{2,1,0:T(8,128)(2,1)}), bf16[8,96,768]{2,1,0:T(8,128)(2,1)}, u32[]{:S(2)}, u32[]{:S(2)}) async-start(bf16[8,96,768]{2,1,0:T(8,128)(2,1)} %bitcast.313), calls=%async_computation.1 | async-start | bytes 2359296 | tf_op jit(solution)/shard_map/all_to_all | solution.py:117
  234.6 340.4 %all-reduce.8.cloned.1.call-start = ((), (), s32[]{:S(2)}) async-start(), calls=%async_computation.9 | async-start | bytes 18874368 | tf_op jit(solution)/shard_map/psum | solution.py:220
  246.4 526.4 %all-reduce.6.cloned.1.call-start = ((), (), s32[]{:S(2)}) async-start(), calls=%async_computation.8 | async-start | bytes 18874368 | tf_op jit(solution)/shard_map/psum | solution.py:208
  249.7 4.5 copy-start.81
  256.9 3.1 copy-start.86
  260.6 4.4 copy-start.88
  265.0 4.2 copy-start.29
  269.3 3.7 copy-start.6
  277.9 5.7 slice-start
  277.9 5.7 slice-start.1
  288.2 7.2 slice-start.2
  291.0 4.5 slice-start.3
  321.8 3.2 copy-start.83
  321.8 3.2 copy-start.84
  321.8 53.0 %copy-start.80 = (f32[384]{0:T(512)S(1)}, f32[384]{0:T(512)}, u32[]{:S(2)}) copy-start(f32[384]{0:T(512)} %copy-done.79) | copy-start | bytes 4612
  372.2 3.2 copy-start.8
  372.2 3.2 copy-start.36
  575.1 7.5 copy-start.25
  772.8 3.4 copy-start.46
  (61 other events, 108.2 us)
Sparse Core Ops, SparseCore 0:
  246.5 328.4 all-reduce.7
  581.9 190.9 all-reduce.5
where the time goes:
time: 799 us; the launch traced here: 790 us
  waiting for transfers between devices  397 us (50%)
  matrix products  184 us (23%)
  local copies, waits for them, and re-layouts  61.3 us (8%)
  other arithmetic  49.6 us (6%)
  blocking collectives  46.7 us (6%)
  starting transfers between devices  35.6 us (4%)
  between operations  15.4 us (2%)
    psum x1, waiting for transfers between devices, per_device(): lax.psum(grad_in_sum.astype(jnp.bfloat16), 'dp').astype(jnp.float32)  197 us
    psum x1, waiting for transfers between devices, per_device(): lax.psum((dense_total[0], dense_total[1], dense_total[2], dense_total[3],...  185 us
    psum x1, blocking collectives, per_device(): lax.psum((dense_total[0], dense_total[1], dense_total[2], dense_total[3],...  46.7 us
    dot_general x2, matrix products, per_device(): jnp.dot(active.T, grad_recv, preferred_element_type=float_type)  25.3 us
    dot_general x2, matrix products, per_device(): jnp.dot(received.T, grad_pre, preferred_element_type=float_type)  21.9 us
    dot_general x2, matrix products, per_device(): pre_active = jnp.dot(received, weight_in, preferred_element_type=float_type)  21.1 us
    unnamed x202, local copies, waits for them, and re-layouts  20.3 us
    dot_general x2, matrix products, per_device(): jnp.dot(active, weight_out, preferred_element_type=float_type)  19.7 us
  transfers between devices with their start and end apart: 10, of which 4 were waited for; matrix products, arithmetic and copies ran while one was open for 31% of the time, Pallas kernels for 0%

commit v1 on v0

--- a/solution.py
+++ b/solution.py
@@ -206,15 +206,18 @@
         )
         dense_total = tuple((total + term for total, term in zip(dense_total, terms)))
     dense_total = lax.psum(
-        (
-            dense_total[0],
-            dense_total[1],
-            dense_total[2],
-            dense_total[3],
-            dense_total[4],
-            dense_total[5],
+        lax.psum(
+            (
+                dense_total[0],
+                dense_total[1],
+                dense_total[2],
+                dense_total[3],
+                dense_total[4],
+                dense_total[5],
+            ),
+            "expert",
         ),
-        ("dp", "expert"),
+        "dp",
     )
     expert_in_sum, expert_out_sum = (
         lax.psum(grad_in_sum.astype(jnp.bfloat16), "dp").astype(jnp.float32),

time: 799 us -> 1110 us (1.39)
  waiting for transfers between devices: 397 us -> 734 us
  blocking collectives: 46.7 us -> 27.6 us
    psum x0 -> x1, waiting for transfers between devices: none -> 317 us  [per_device(): lax.psum(lax.psum((dense_total[0], dense_total[1], dense_total[2], dense_...]
    psum x1, waiting for transfers between devices: 197 us -> 284 us  [per_device(): lax.psum(grad_in_sum.astype(jnp.bfloat16), 'dp').astype(jnp.float32)]
    psum x1, waiting for transfers between devices: 185 us -> 108 us  [per_device(): lax.psum((dense_total[0], dense_total[1], dense_total[2], dense_total[3],...]
    psum x1, blocking collectives: 46.7 us -> 14.5 us  [per_device(): lax.psum((dense_total[0], dense_total[1], dense_total[2], dense_total[3],...]
    psum x0 -> x1, blocking collectives: none -> 13.1 us  [per_device(): lax.psum(lax.psum((dense_total[0], dense_total[1], dense_total[2], dense_...]
  transfers between devices with their start and end apart: 10 -> 11, of which waited for: 4 -> 8; matrix products, arithmetic and copies ran while one was open for 31% -> 17% of each run, Pallas kernels for 0% -> 0%
where the time goes in v1:
time: 1110 us; the launch traced here: 1100 us
  waiting for transfers between devices  734 us (66%)
  matrix products  177 us (16%)
  local copies, waits for them, and re-layouts  64.9 us (6%)
  other arithmetic  50.8 us (5%)
  starting transfers between devices  34 us (3%)
  blocking collectives  27.6 us (2%)
  between operations  15.1 us (1%)
    psum x1, waiting for transfers between devices, per_device(): lax.psum(lax.psum((dense_total[0], dense_total[1], dense_total[2], dense_...  317 us
    psum x1, waiting for transfers between devices, per_device(): lax.psum(grad_in_sum.astype(jnp.bfloat16), 'dp').astype(jnp.float32)  284 us
    psum x1, waiting for transfers between devices, per_device(): lax.psum((dense_total[0], dense_total[1], dense_total[2], dense_total[3],...  108 us
  transfers between devices with their start and end apart: 11, of which 8 were waited for; matrix products, arithmetic and copies ran while one was open for 17% of the time, Pallas kernels for 0%

profile of v1, /device:TPU:0, one launch (start us, length us, event | category | flops | bytes accessed | tf_op | source)
XLA Modules:
  0.0 1103.7 jit_solution(1266242767041159547)
XLA Ops:
  18.3 3.0 convolution_convert_fusion.10
  36.7 3.9 scatter_custom_fusion
  40.7 5.4 all-to-all-start
  50.4 3.7 scatter_custom_fusion.2
  68.7 3.8 scatter_custom_fusion.3
  72.6 5.0 convolution_convert_fusion
  79.1 3.2 scatter_custom_fusion.1
  82.3 4.2 all-to-all-start.4
  86.5 12.6 %multiply_convert_fusion.3 = (bf16[768,3072]{1,0:T(8,128)(2,1)}, f32[768,3072]{1,0:T(8,128)}) fusion(bf16[768,768]{1,0:T(8,128)(2,1)} %bitcast.13, bf16[1,768,3072]{2,1,0:T(8,128)(2,1)} %param.28), kind=kOutput, calls=%fused_computation.16 | convolution fusion | flops 3635675136 | bytes 20054016 | tf_op jit(solution)/shard_map/dot_general | solution.py:114
  99.1 4.2 all-to-all-done.4
  103.3 3.6 all-to-all-start.2
  106.9 10.2 multiply_convert_fusion.1
  117.1 6.5 all-to-all-done.2
  123.7 4.8 all-to-all-start.6
  128.5 8.7 fusion.12
  137.2 7.2 fusion.20
  145.3 3.6 all-to-all-start.5
  148.8 8.9 multiply_convert_fusion
  159.8 7.2 fusion.23
  167.0 4.3 all-to-all-start.7
  171.3 11.3 %fusion.29 = bf16[768,768]{1,0:T(8,128)(2,1)} fusion(bf16[1,3072,768]{2,1,0:T(8,128)(2,1)} %param.29, f32[768,3072]{1,0:T(8,128)} %fusion.12), kind=kOutput, calls=%fused_computation.59 | convolution fusion | flops 3636264960 | bytes 15335424 | tf_op jit(solution)/shard_map/dot_general | solution.py:116
  182.6 5.5 all-to-all-done.7
  189.1 4.3 all-to-all-start.3
  193.4 8.6 fusion.26
  202.0 8.2 all-to-all-done.3
  210.2 3.6 all-to-all-start.1
  216.0 4.6 gather_fusion.5
  220.6 4.6 gather_fusion.3
  225.2 2.6 gather_fusion.4
  227.8 3.4 fusion.60
  232.4 2.6 gather_fusion.1
  235.1 4.2 fusion.70
  242.9 5.9 multiply_reduce_fusion
  254.9 2.8 convolution_convert_fusion.2
  261.4 5.7 multiply_reduce_fusion.1
  287.9 6.4 fusion.144
  294.3 9.6 fusion.145
  303.8 8.1 fusion.16
  312.0 9.3 fusion.17
  321.4 107.6 %all-reduce.9.cloned.1.call-done = (f32[768,768]{1,0:T(8,128)}, f32[768,768]{1,0:T(8,128)}, f32[768,768]{1,0:T(8,128)}, f32[768,768]{1,0:T(8,128)}) async-done(((f32[768,768]{1,0:T(8,128)}, f32[768,768]{1,0:T(8,128)}, f32[768,768]{1,0:T(8,128)}, f32[768,768]{1,0:T(8,128)}), (f32[768,768]{1,0:T(8,128)}, f32[768,768]{1,0:T(8,128)}, f32[768,768]{1,0:T(8,128)}, ...) | async-done | bytes 9437200 | tf_op jit(solution)/shard_map/psum | solution.py:209
  436.4 2.6 fusion.57
  440.2 14.5 %all-reduce = (f32[768]{0:T(1024)}, f32[768]{0:T(1024)}) all-reduce(f32[768]{0:T(1024)} %add.219, f32[768]{0:T(1024)} %add.220), channel_id=1, replica_groups=mesh['dp'=4,'expert'=8] {'expert'}, use_global_device_ids=true, to_apply=%region_34.37 | all-reduce | flops 1536 | bytes 12288 | tf_op jit(solution)/shard_map/psum | solution.py:209
  454.6 13.1 %all-reduce.2 = (f32[768]{0:T(1024)}, f32[768]{0:T(1024)}) all-reduce(f32[768]{0:T(1024)} %get-tuple-element.28, f32[768]{0:T(1024)} %get-tuple-element.29), channel_id=1, replica_groups=mesh['dp'=4,'expert'=8] {'dp'}, use_global_device_ids=true, to_apply=%region_35.38 | all-reduce | flops 1536 | bytes 12288 | tf_op jit(solution)/shard_map/psum | solution.py:208
  474.0 284.3 %all-reduce.13.cloned.1.call-done = (bf16[1,768,3072]{2,1,0:T(8,128)(2,1)}, bf16[1,3072,768]{2,1,0:T(8,128)(2,1)}) async-done(((bf16[1,768,3072]{2,1,0:T(8,128)(2,1)}, bf16[1,3072,768]{2,1,0:T(8,128)(2,1)}), (bf16[1,768,3072]{2,1,0:T(8,128)(2,1)}, bf16[1,3072,768]{2,1,0:T(8,128)(2,1)})) %all-reduce.13.cloned.1.call-update) | async-done | bytes 9437200 | tf_op jit(solution)/shard_map/psum | solution.py:223
  758.3 7.5 broadcast_in_dim.117
  765.9 4.5 broadcast_in_dim.119
  770.3 316.8 %all-reduce.11.cloned.1.call-done = (f32[768,768]{1,0:T(8,128)}, f32[768,768]{1,0:T(8,128)}, f32[768,768]{1,0:T(8,128)}, f32[768,768]{1,0:T(8,128)}) async-done(((f32[768,768]{1,0:T(8,128)}, f32[768,768]{1,0:T(8,128)}, f32[768,768]{1,0:T(8,128)}, f32[768,768]{1,0:T(8,128)}), (f32[768,768]{1,0:T(8,128)}, f32[768,768]{1,0:T(8,128)}, f32[768,768]{1,0:T(8,128)}, ...) | async-done | bytes 9437200 | tf_op jit(solution)/shard_map/psum | solution.py:208
  1087.2 3.4 copy.73
  (292 shorter events, 109.3 us)
Async XLA Ops:
  8.9 37.1 %copy-start.74 = (f32[384]{0:T(512)}, f32[384]{0:T(512)S(1)}, u32[]{:S(2)}) copy-start(f32[384]{0:T(512)S(1)} %get-tuple-element.23) | copy-start | bytes 4612
  9.5 8.8 copy-start.68
  11.0 4.4 copy-start.30
  18.3 4.4 copy-start.11
  31.7 5.0 copy-start.67
  36.7 13.7 %copy-start.81 = (s32[384]{0:T(512)}, s32[384]{0:T(512)S(1)}, u32[]{:S(2)}) copy-start(s32[384]{0:T(512)S(1)} %get-tuple-element.43) | copy-start | bytes 4612
  40.7 41.7 %all-to-all-start = ((bf16[8,96,768]{2,1,0:T(8,128)(2,1)}), bf16[8,96,768]{2,1,0:T(8,128)(2,1)}, u32[]{:S(2)}, u32[]{:S(2)}) async-start(bf16[8,96,768]{2,1,0:T(8,128)(2,1)} %bitcast.301), calls=%async_computation | async-start | bytes 2359296 | tf_op jit(solution)/shard_map/all_to_all | solution.py:111
  50.4 4.7 copy-start.76
  55.2 17.3 %copy-start.39 = (pred[384,384]{0,1:T(8,128)(4,1)}, pred[384,384]{0,1:T(8,128)(4,1)S(1)}, u32[]{:S(2)}) copy-start(pred[384,384]{0,1:T(8,128)(4,1)S(1)} %fusion.96) | copy-start | bytes 442372
  56.7 4.7 copy-start.15
  64.3 8.2 copy-start.63
  66.9 5.6 copy-start.48
  68.7 10.4 copy-start.84
  72.6 5.0 copy-start.27
  78.5 3.8 copy-start.10
  82.3 21.0 %all-to-all-start.4 = ((bf16[8,96,768]{2,1,0:T(8,128)(2,1)}), bf16[8,96,768]{2,1,0:T(8,128)(2,1)S(1)}, u32[]{:S(2)}, u32[]{:S(2)}) async-start(bf16[8,96,768]{2,1,0:T(8,128)(2,1)} %bitcast.37), calls=%async_computation.4 | async-start | bytes 2359296 | tf_op jit(solution)/shard_map/all_to_all | solution.py:133
  103.3 3.6 copy-start.51
  103.3 20.3 %all-to-all-start.2 = ((bf16[8,96,768]{2,1,0:T(8,128)(2,1)}), bf16[8,96,768]{2,1,0:T(8,128)(2,1)S(1)}, u32[]{:S(2)}, u32[]{:S(2)}) async-start(bf16[8,96,768]{2,1,0:T(8,128)(2,1)} %bitcast.31), calls=%async_computation.2 | async-start | bytes 2359296 | tf_op jit(solution)/shard_map/all_to_all | solution.py:111
  123.6 4.8 copy-start.53
  123.6 13.5 %slice-start.4 = ((s8[4718592]{0:T(1024)(128)(4,1)}), s8[524288]{0:T(1024)(128)(4,1)S(1)}, s32[]{:S(2)}) async-start(s8[4718592]{0:T(1024)(128)(4,1)} %bitcast.302), calls=%async_computation.15 | async-start | bytes 1048576
  123.7 21.6 %all-to-all-start.6 = ((bf16[8,96,768]{2,1,0:T(8,128)(2,1)}), bf16[8,96,768]{2,1,0:T(8,128)(2,1)}, u32[]{:S(2)}, u32[]{:S(2)}) async-start(bf16[8,96,768]{2,1,0:T(8,128)(2,1)} %bitcast.55), calls=%async_computation.6 | async-start | bytes 2359296 | tf_op jit(solution)/shard_map/all_to_all | solution.py:133
  128.5 8.7 slice-start.5
  145.3 21.7 %all-to-all-start.5 = ((bf16[8,96,768]{2,1,0:T(8,128)(2,1)}), bf16[8,96,768]{2,1,0:T(8,128)(2,1)S(1)}, u32[]{:S(2)}, u32[]{:S(2)}) async-start(bf16[8,96,768]{2,1,0:T(8,128)(2,1)} %bitcast.39), calls=%async_computation.5 | async-start | bytes 2359296 | tf_op jit(solution)/shard_map/all_to_all | solution.py:145
  167.0 21.1 %all-to-all-start.7 = ((bf16[8,96,768]{2,1,0:T(8,128)(2,1)}), bf16[8,96,768]{2,1,0:T(8,128)(2,1)S(1)}, u32[]{:S(2)}, u32[]{:S(2)}) async-start(bf16[8,96,768]{2,1,0:T(8,128)(2,1)} %bitcast.320), calls=%async_computation.7 | async-start | bytes 2359296 | tf_op jit(solution)/shard_map/all_to_all | solution.py:145
  189.1 21.1 %all-to-all-start.3 = ((bf16[8,96,768]{2,1,0:T(8,128)(2,1)}), bf16[8,96,768]{2,1,0:T(8,128)(2,1)}, u32[]{:S(2)}, u32[]{:S(2)}) async-start(bf16[8,96,768]{2,1,0:T(8,128)(2,1)} %bitcast.319), calls=%async_computation.3 | async-start | bytes 2359296 | tf_op jit(solution)/shard_map/all_to_all | solution.py:117
  210.2 22.2 %all-to-all-start.1 = ((bf16[8,96,768]{2,1,0:T(8,128)(2,1)}), bf16[8,96,768]{2,1,0:T(8,128)(2,1)S(1)}, u32[]{:S(2)}, u32[]{:S(2)}) async-start(bf16[8,96,768]{2,1,0:T(8,128)(2,1)} %bitcast.318), calls=%async_computation.1 | async-start | bytes 2359296 | tf_op jit(solution)/shard_map/all_to_all | solution.py:117
  213.8 215.2 %all-reduce.9.cloned.1.call-start = ((), (), s32[]{:S(2)}) async-start(), calls=%async_computation.8 | async-start | bytes 18874368 | tf_op jit(solution)/shard_map/psum | solution.py:209
  227.8 3.4 copy-start.80
  227.8 4.0 copy-start.83
  235.1 4.2 copy-start.28
  239.2 18.5 %copy-start.7 = (f32[384,768]{1,0:T(8,128)}, f32[384,768]{1,0:T(8,128)S(1)}, u32[]{:S(2)}) copy-start(f32[384,768]{1,0:T(8,128)S(1)} %get-tuple-element.48) | copy-start | bytes 3538948
  242.9 5.9 slice-start.2
  242.9 5.9 slice-start.3
  242.9 5.9 copy-start.40
  242.9 5.9 copy-start.64
  261.4 5.7 slice-start
  261.4 5.7 slice-start.1
  270.7 4.3 copy-start.23
  272.1 4.5 copy-start.21
  287.8 470.5 %all-reduce.13.cloned.1.call-start = ((), (), s32[]{:S(2)}) async-start(), calls=%async_computation.10 | async-start | bytes 18874368 | tf_op jit(solution)/shard_map/psum | solution.py:223
  287.9 6.4 copy-start.52
  294.2 9.6 copy-start.54
  294.3 17.7 %slice-start.6 = ((s8[9437184]{0:T(1024)(128)(4,1)}), s8[4194304]{0:T(1024)(128)(4,1)S(1)}, s32[]{:S(2)}) async-start(s8[9437184]{0:T(1024)(128)(4,1)} %bitcast.331), calls=%async_computation.17 | async-start | bytes 8388608
  294.3 17.7 %slice-start.7 = ((s8[9437184]{0:T(1024)(128)(4,1)}), s8[4194304]{0:T(1024)(128)(4,1)S(1)}, s32[]{:S(2)}) async-start(s8[9437184]{0:T(1024)(128)(4,1)} %bitcast.331), calls=%async_computation.18 | async-start | bytes 8388608
  303.8 8.1 slice-start.8
  321.3 765.8 %all-reduce.11.cloned.1.call-start = ((), (), s32[]{:S(2)}) async-start(), calls=%async_computation.9 | async-start | bytes 18874368 | tf_op jit(solution)/shard_map/psum | solution.py:208
  436.4 33.9 %copy-start.75 = (f32[384]{0:T(512)S(1)}, f32[384]{0:T(512)}, u32[]{:S(2)}) copy-start(f32[384]{0:T(512)} %copy-done.74) | copy-start | bytes 4612
  758.3 7.5 copy-start.25
  (59 other events, 121.5 us)
Sparse Core Ops, SparseCore 0:
  287.9 141.0 all-reduce.8
  432.4 325.9 all-reduce.12
  761.4 325.6 all-reduce.10
